TPU v7x, 256 devices: a whole 4x4x8 slice. The times are simulated.
256 devices in a mesh: row: 16 (over x, z_lo, core), col: 16 (over y, z_hi).
Axes of the slice: x: 4, y: 4, z: 8 (z_hi: 4, z_lo: 2; z = z_hi * 2 + z_lo), core: 2. Of those that a mesh axis runs over, the one named last changes fastest.
Arguments:
- dosage: bfloat16 [1536, 196608], P(None, ('row', 'col')), may hold values from 0 to 2
- zscores: bfloat16 [196608], P(('row', 'col')), may hold values from -18 to 18
- band_reach: int32 [256], replicated, may hold values from 0 to 2, as said below
Outputs:
- ld_tiles: bfloat16 [196608, 3840], P(('row', 'col'))
- smoothed: float32 [196608], P(('row', 'col'))
- quadratic: float32 [], replicated
Inputs may be any that keep to these rules, and one draw needn't show every extreme that they name: `band_reach`: the first 3 blocks, the last 3 blocks and some two neighbouring blocks reach 2.
All inputs are finite; a program needn't handle non-finite values.
Results may differ from a plain program's by a relative error of at most 0.0042.
Values may be sent and summed in bfloat16 or wider, within the bound.
A program may use at most 64 MiB of HBM per device.

v0:
```python
import jax
import jax.numpy as jnp
from jax import lax
from jax.sharding import Mesh
from jax.sharding import PartitionSpec as P

BAND = 2
ROW_COL = ("row_0", "row_1", "row_2", "col_0", "col_1")


def passed_along(value, axis, steps):
    count = lax.axis_size(axis)
    initial, last = (max(0, -steps), min(count, count - steps))
    return lax.ppermute(value, axis, [(source, source + steps) for source in range(initial, last)])


def by_axis(value, axes):
    for axis in axes:
        value = lax.psum(value, axis)
    return value


def standardize(dosage):
    values = dosage.astype(jnp.float32)
    column_mean = jnp.mean(values, axis=0)
    centered = values - column_mean
    variance = jnp.mean(centered * centered, axis=0)
    return (centered * lax.rsqrt(variance + 1e-05)).astype(jnp.bfloat16)


def body(dosage, zscores, band_reach):
    samples = dosage.shape[0]
    block_width = zscores.shape[0]
    block_count = lax.axis_size(ROW_COL)
    position = lax.axis_index(ROW_COL)
    scaled = standardize(dosage)
    own_reach = lax.dynamic_index_in_dim(band_reach, position, 0, False)

    def allowed(offset):
        other = position + offset
        inside = (other >= 0) & (other < block_count)
        their_reach = lax.dynamic_index_in_dim(
            band_reach, jnp.clip(other, 0, block_count - 1), 0, False
        )
        return inside & (abs(offset) <= jnp.minimum(own_reach, their_reach))

    def make_tile(left, right, offset):
        product = (
            lax.dot_general(
                left, right, (((0,), (0,)), ((), ())), preferred_element_type=jnp.float32
            )
            / samples
        )
        return jnp.where(allowed(offset), product, 0.0).astype(jnp.bfloat16)

    def apply_tile(ld_tile, near_scores):
        return jnp.dot(ld_tile, near_scores, preferred_element_type=jnp.float32)

    own_z = zscores.astype(jnp.float32)
    tile_map = {0: make_tile(scaled, scaled, 0)}
    score_map = {0: zscores}
    for offset in range(1, BAND + 1):
        far_scaled, far_z = passed_along((scaled, zscores), ROW_COL, -offset)
        tile_map[offset] = make_tile(scaled, far_scaled, offset)
        score_map[offset] = far_z
    terms = {}
    for offset in range(0, BAND + 1):
        terms[offset] = apply_tile(tile_map[offset], score_map[offset])
    total = None
    for offset in range(1, BAND + 1):
        returned, returned_z = passed_along((tile_map[offset], zscores), ROW_COL, offset)
        tile_map[-offset] = returned.T
        score_map[-offset] = returned_z
    for offset in range(1, BAND + 1):
        terms[-offset] = apply_tile(tile_map[-offset], score_map[-offset])
    smoothed = terms[0]
    for offset in range(1, BAND + 1):
        smoothed = smoothed + terms[offset] + terms[-offset]
    total = by_axis(jnp.sum(own_z * smoothed), ROW_COL)
    quadratic = total / (block_count * block_width)
    ld_tiles = jnp.concatenate([tile_map[offset] for offset in range(-BAND, BAND + 1)], axis=1)
    return (ld_tiles, smoothed, quadratic)


def solution(mesh):
    torus = Mesh(mesh.devices.reshape(4, 2, 2, 4, 4), ("row_0", "row_1", "row_2", "col_0", "col_1"))
    return jax.shard_map(
        body,
        mesh=torus,
        in_specs=(P(None, ROW_COL), P(ROW_COL), P()),
        out_specs=(P(ROW_COL, None), P(ROW_COL), P()),
        check_vma=False,
    )
```

profile of v0, /device:TPU:2, one launch (start us, length us, event | category | flops | bytes accessed | tf_op | source)
XLA Modules:
  0.0 394.4 jit_solution(10155190319292497556)
XLA Ops:
  0.6 2.2 convert_reduce_fusion
  3.7 2.0 fusion.3
  5.7 9.6 %collective-permute-start.2 = (bf16[1536,768]{1,0:T(8,128)(2,1)}, bf16[1536,768]{1,0:T(8,128)(2,1)S(1)}, u32[]{:S(2)}, u32[]{:S(2)}) collective-permute-start(bf16[1536,768]{1,0:T(8,128)(2,1)} %fusion.3), channel_id=1, source_target_pairs={{1,0},{2,1},{3,2},{4,3},{5,4},{6,5},{7,6},{8,7},{9,8},{10,9},{11,1... | collective-permute-start | bytes 7077896 | tf_op jit(solution)/shard_map/ppermute | solution.py:14
  15.3 3.1 collective-permute-start
  21.5 210.7 %collective-permute-done.2 = bf16[1536,768]{1,0:T(8,128)(2,1)S(1)} collective-permute-done((bf16[1536,768]{1,0:T(8,128)(2,1)}, bf16[1536,768]{1,0:T(8,128)(2,1)S(1)}, u32[]{:S(2)}, u32[]{:S(2)}) %collective-permute-start.2) | collective-permute-done | bytes 2359328 | tf_op jit(solution)/shard_map/ppermute | solution.py:14
  232.2 3.7 select_convert_fusion.1
  235.9 1.9 collective-permute-start.3
  237.8 46.4 %collective-permute-done = bf16[1536,768]{1,0:T(8,128)(2,1)} collective-permute-done((bf16[1536,768]{1,0:T(8,128)(2,1)}, bf16[1536,768]{1,0:T(8,128)(2,1)}, u32[]{:S(2)}, u32[]{:S(2)}) %collective-permute-start) | collective-permute-done | bytes 2359328 | tf_op jit(solution)/shard_map/ppermute | solution.py:14
  284.2 4.4 %select_convert_fusion.2 = bf16[768,768]{0,1:T(8,128)(2,1)S(1)} fusion(bf16[1536,768]{1,0:T(8,128)(2,1)} %fusion.3, bf16[1536,768]{1,0:T(8,128)(2,1)} %collective-permute-done, pred[]{:T(512)S(6)} %and.24), kind=kOutput, calls=%fused_computation.8 | convolution fusion | flops 1813708800 | bytes 5898241 | tf_op jit(solution)/shard_map/dot_general | solution.py:49
  290.1 1.9 collective-permute-start.1
  292.0 9.8 %collective-permute-start.6 = (bf16[768]{0:T(1024)(128)(2,1)S(1)}, bf16[768]{0:T(1024)(128)(2,1)S(1)}, u32[]{:S(2)}, u32[]{:S(2)}) collective-permute-start(bf16[768]{0:T(1024)(128)(2,1)S(1)} %copy-done.3), channel_id=1, source_target_pairs={{2,0},{3,1},{4,2},{5,3},{6,4},{7,5},{8,6},{9,7},{10,8},{11,9},{12,... | collective-permute-start | bytes 4616 | tf_op jit(solution)/shard_map/ppermute | solution.py:14
  301.9 1.9 collective-permute-start.5
  303.8 7.9 %collective-permute-start.4 = (bf16[768]{0:T(1024)(128)(2,1)S(1)}, bf16[768]{0:T(1024)(128)(2,1)}, u32[]{:S(2)}, u32[]{:S(2)}) collective-permute-start(bf16[768]{0:T(1024)(128)(2,1)S(1)} %copy-done.3), channel_id=1, source_target_pairs={{1,0},{2,1},{3,2},{4,3},{5,4},{6,5},{7,6},{8,7},{9,8},{10,9},{11,1... | collective-permute-start | bytes 4616 | tf_op jit(solution)/shard_map/ppermute | solution.py:14
  311.7 1.9 collective-permute-start.7
  315.7 7.0 %collective-permute-done.7 = bf16[768]{0:T(1024)(128)(2,1)} collective-permute-done((bf16[768]{0:T(1024)(128)(2,1)S(1)}, bf16[768]{0:T(1024)(128)(2,1)}, u32[]{:S(2)}, u32[]{:S(2)}) %collective-permute-start.7) | collective-permute-done | bytes 1568 | tf_op jit(solution)/shard_map/ppermute | solution.py:14
  326.0 2.5 bitcast_dynamic-update-slice_fusion
  329.6 5.4 %constant_dynamic-update-slice_fusion.2 = (bf16[768,3840]{0,1:T(8,128)(2,1)}, bf16[768,768]{0,1:T(8,128)(2,1)S(1)}) fusion(bf16[768,3840]{0,1:T(8,128)(2,1)} %constant_dynamic-update-slice_fusion.3, bf16[1536,768]{1,0:T(8,128)(2,1)} %fusion.3, pred[]{:T(512)S(6)} %and.28), kind=kOutput, calls=%fused_computation.19 | convolution fusion | flops 1813708800 | bytes 7077889 | tf_op jit(solution)/shard_map/dot_general | solution.py:49
  335.8 1.6 fusion.6
  338.6 8.5 %psum.35 = f32[]{:T(128)} all-reduce(f32[]{:T(128)} %get-tuple-element.6), channel_id=1, replica_groups=mesh['row_0'=4,'row_1'=2,'row_2'=2,'col_0'=4,'col_1'=4] {'row_0'}, use_global_device_ids=true, to_apply=%region_3.4 | all-reduce | flops 1 | bytes 8 | tf_op jit(solution)/shard_map/psum | solution.py:19
  347.0 5.5 %psum.36 = f32[]{:T(128)} all-reduce(f32[]{:T(128)} %psum.35), channel_id=1, replica_groups=mesh['row_0'=4,'row_1'=2,'row_2'=2,'col_0'=4,'col_1'=4] {'row_1'}, use_global_device_ids=true, to_apply=%region_4.5 | all-reduce | flops 1 | bytes 8 | tf_op jit(solution)/shard_map/psum | solution.py:19
  353.7 3.1 psum.37
  357.9 8.4 %psum.38 = f32[]{:T(128)} all-reduce(f32[]{:T(128)} %psum.37), channel_id=1, replica_groups=mesh['row_0'=4,'row_1'=2,'row_2'=2,'col_0'=4,'col_1'=4] {'col_0'}, use_global_device_ids=true, to_apply=%region_6.7 | all-reduce | flops 1 | bytes 8 | tf_op jit(solution)/shard_map/psum | solution.py:19
  366.3 8.4 %copy.8 = bf16[768,3840]{1,0:T(8,128)(2,1)} copy(bf16[768,3840]{0,1:T(8,128)(2,1)} %constant_dynamic-update-slice_fusion) | data formatting | bytes 11796480
  374.7 17.9 %psum.39 = f32[]{:T(128)} all-reduce(f32[]{:T(128)} %psum.38), channel_id=1, replica_groups=mesh['row_0'=4,'row_1'=2,'row_2'=2,'col_0'=4,'col_1'=4] {'col_1'}, use_global_device_ids=true, to_apply=%region_7.8 | all-reduce | flops 1 | bytes 8 | tf_op jit(solution)/shard_map/psum | solution.py:19
  (36 shorter events, 12.3 us)
Async XLA Ops:
  0.6 2.4 copy-start
  3.7 14.7 %copy-start.5 = (s32[256]{0:T(256)S(1)}, s32[256]{0:T(256)}, u32[]{:S(2)}) copy-start(s32[256]{0:T(256)} %param.5) | copy-start | bytes 3076
  5.7 226.5 %collective-permute-start.2 = (bf16[1536,768]{1,0:T(8,128)(2,1)}, bf16[1536,768]{1,0:T(8,128)(2,1)S(1)}, u32[]{:S(2)}, u32[]{:S(2)}) collective-permute-start(bf16[1536,768]{1,0:T(8,128)(2,1)} %fusion.3), channel_id=1, source_target_pairs={{1,0},{2,1},{3,2},{4,3},{5,4},{6,5},{7,6},{8,7},{9,8},{10,9},{11,1... | collective-permute-start | bytes 7077896 | tf_op jit(solution)/shard_map/ppermute | solution.py:14
  15.3 268.9 %collective-permute-start = (bf16[1536,768]{1,0:T(8,128)(2,1)}, bf16[1536,768]{1,0:T(8,128)(2,1)}, u32[]{:S(2)}, u32[]{:S(2)}) collective-permute-start(bf16[1536,768]{1,0:T(8,128)(2,1)} %fusion.3), channel_id=1, source_target_pairs={{2,0},{3,1},{4,2},{5,3},{6,4},{7,5},{8,6},{9,7},{10,8},{11,9},{12,... | collective-permute-start | bytes 7077896 | tf_op jit(solution)/shard_map/ppermute | solution.py:14
  235.9 88.6 %collective-permute-start.3 = (bf16[768,768]{0,1:T(8,128)(2,1)S(1)}, bf16[768,768]{0,1:T(8,128)(2,1)S(1)}, u32[]{:S(2)}, u32[]{:S(2)}) collective-permute-start(bf16[768,768]{0,1:T(8,128)(2,1)S(1)} %select_convert_fusion.1), channel_id=1, source_target_pairs={{0,1},{1,2},{2,3},{3,4},{4,5},{5,6},{6,7},{7,8},{8,9},{9,10},{10,1... | collective-permute-start | bytes 3538952 | tf_op jit(solution)/shard_map/ppermute | solution.py:14
  288.6 3.4 copy-start.3
  290.1 35.9 %collective-permute-start.1 = (bf16[768,768]{1,0:T(8,128)(2,1)}, bf16[768,768]{1,0:T(8,128)(2,1)}, u32[]{:S(2)}, u32[]{:S(2)}) collective-permute-start(bf16[768,768]{1,0:T(8,128)(2,1)} %copy.6), channel_id=1, source_target_pairs={{0,2},{1,3},{2,4},{3,5},{4,6},{5,7},{6,8},{7,9},{8,10},{9,11},{10,... | collective-permute-start | bytes 3538952 | tf_op jit(solution)/shard_map/ppermute | solution.py:14
  292.0 19.6 %collective-permute-start.6 = (bf16[768]{0:T(1024)(128)(2,1)S(1)}, bf16[768]{0:T(1024)(128)(2,1)S(1)}, u32[]{:S(2)}, u32[]{:S(2)}) collective-permute-start(bf16[768]{0:T(1024)(128)(2,1)S(1)} %copy-done.3), channel_id=1, source_target_pairs={{2,0},{3,1},{4,2},{5,3},{6,4},{7,5},{8,6},{9,7},{10,8},{11,9},{12,... | collective-permute-start | bytes 4616 | tf_op jit(solution)/shard_map/ppermute | solution.py:14
  301.9 13.2 %collective-permute-start.5 = (bf16[768]{0:T(1024)(128)(2,1)S(1)}, bf16[768]{0:T(1024)(128)(2,1)S(1)}, u32[]{:S(2)}, u32[]{:S(2)}) collective-permute-start(bf16[768]{0:T(1024)(128)(2,1)S(1)} %copy-done.3), channel_id=1, source_target_pairs={{0,1},{1,2},{2,3},{3,4},{4,5},{5,6},{6,7},{7,8},{8,9},{9,10},{10,1... | collective-permute-start | bytes 4616 | tf_op jit(solution)/shard_map/ppermute | solution.py:14
  303.8 11.2 %collective-permute-start.4 = (bf16[768]{0:T(1024)(128)(2,1)S(1)}, bf16[768]{0:T(1024)(128)(2,1)}, u32[]{:S(2)}, u32[]{:S(2)}) collective-permute-start(bf16[768]{0:T(1024)(128)(2,1)S(1)} %copy-done.3), channel_id=1, source_target_pairs={{1,0},{2,1},{3,2},{4,3},{5,4},{6,5},{7,6},{8,7},{9,8},{10,9},{11,1... | collective-permute-start | bytes 4616 | tf_op jit(solution)/shard_map/ppermute | solution.py:14
  311.7 11.0 %collective-permute-start.7 = (bf16[768]{0:T(1024)(128)(2,1)S(1)}, bf16[768]{0:T(1024)(128)(2,1)}, u32[]{:S(2)}, u32[]{:S(2)}) collective-permute-start(bf16[768]{0:T(1024)(128)(2,1)S(1)} %copy-done.3), channel_id=1, source_target_pairs={{0,2},{1,3},{2,4},{3,5},{4,6},{5,7},{6,8},{7,9},{8,10},{9,11},{10,... | collective-permute-start | bytes 4616 | tf_op jit(solution)/shard_map/ppermute | solution.py:14
  326.0 2.5 copy-start.1
  335.0 0.8 copy-start.2
  335.0 2.3 copy-start.4
where the time goes:
time: 395 us; the launch traced here: 394 us
  waiting for transfers between devices  264 us (67%)
  blocking collectives  43.4 us (11%)
  starting transfers between devices  38.1 us (10%)
  local copies, waits for them, and re-layouts  19.8 us (5%)
  matrix products  16.4 us (4%)
  between operations  6.27 us (2%)
  other arithmetic  6.11 us (2%)
    ppermute x8, waiting for transfers between devices, passed_along(): lax.ppermute(value, axis, [(source, source + steps) for source in range(i...  264 us
    psum x5, blocking collectives, by_axis(): value = lax.psum(value, axis)  43.4 us
    ppermute x8, starting transfers between devices, passed_along(): lax.ppermute(value, axis, [(source, source + steps) for source in range(i...  38.1 us
    dot_general x3, matrix products, make_tile(): lax.dot_general(left, right, (((0,), (0,)), ((), ())), preferred_element_...  13.6 us
    unnamed x17, local copies, waits for them, and re-layouts  13.2 us
  transfers between devices with their start and end apart: 8, of which 4 were waited for; matrix products, arithmetic and copies ran while one was open for 4% of the time, Pallas kernels for 0%

commit v1 on v0

--- a/solution.py
+++ b/solution.py
@@ -16,7 +16,7 @@
 
 def by_axis(value, axes):
     for axis in axes:
-        value = lax.psum(value, axis)
+        value = jnp.sum(lax.all_gather(value, axis), axis=0)
     return value
 
 

time: 395 us -> 405 us (1.025)
  local copies, waits for them, and re-layouts: 19.8 us -> 33.2 us
    psum x5 -> x0, blocking collectives: 43.4 us -> none  [by_axis(): value = lax.psum(value, axis)]
    unnamed x0 -> x5, blocking collectives: none -> 40.8 us
    unnamed x17 -> x32, local copies, waits for them, and re-layouts: 13.2 us -> 26.6 us
    ppermute x8, waiting for transfers between devices: 264 us -> 260 us  [passed_along(): lax.ppermute(value, axis, [(source, source + steps) for source in range(i...]
  transfers between devices with their start and end apart: 8 -> 8, of which waited for: 4 -> 3; matrix products, arithmetic and copies ran while one was open for 4% -> 5% of each run, Pallas kernels for 0% -> 0%
where the time goes in v1:
time: 405 us; the launch traced here: 404 us
  waiting for transfers between devices  260 us (64%)
  blocking collectives  40.8 us (10%)
  starting transfers between devices  38.1 us (9%)
  local copies, waits for them, and re-layouts  33.2 us (8%)
  matrix products  17.1 us (4%)
  other arithmetic  9.13 us (2%)
  between operations  6.29 us (2%)
    ppermute x8, waiting for transfers between devices, passed_along(): lax.ppermute(value, axis, [(source, source + steps) for source in range(i...  260 us
    unnamed x5, blocking collectives  40.8 us
    ppermute x8, starting transfers between devices, passed_along(): lax.ppermute(value, axis, [(source, source + steps) for source in range(i...  38.1 us
    unnamed x32, local copies, waits for them, and re-layouts  26.6 us
    dot_general x3, matrix products, make_tile(): lax.dot_general(left, right, (((0,), (0,)), ((), ())), preferred_element_...  14.3 us
  transfers between devices with their start and end apart: 8, of which 3 were waited for; matrix products, arithmetic and copies ran while one was open for 5% of the time, Pallas kernels for 0%

profile of v1, /device:TPU:2, one launch (start us, length us, event | category | flops | bytes accessed | tf_op | source)
XLA Modules:
  0.0 404.3 jit_solution(126198414085689906)
XLA Ops:
  0.6 2.2 convert_reduce_fusion
  3.7 2.0 fusion.3
  5.7 9.6 %collective-permute-start.2 = (bf16[1536,768]{1,0:T(8,128)(2,1)}, bf16[1536,768]{1,0:T(8,128)(2,1)}, u32[]{:S(2)}, u32[]{:S(2)}) collective-permute-start(bf16[1536,768]{1,0:T(8,128)(2,1)} %fusion.3), channel_id=1, source_target_pairs={{1,0},{2,1},{3,2},{4,3},{5,4},{6,5},{7,6},{8,7},{9,8},{10,9},{11,1... | collective-permute-start | bytes 7077896 | tf_op jit(solution)/shard_map/ppermute | solution.py:14
  15.3 3.1 collective-permute-start
  21.5 210.7 %collective-permute-done.2 = bf16[1536,768]{1,0:T(8,128)(2,1)} collective-permute-done((bf16[1536,768]{1,0:T(8,128)(2,1)}, bf16[1536,768]{1,0:T(8,128)(2,1)}, u32[]{:S(2)}, u32[]{:S(2)}) %collective-permute-start.2) | collective-permute-done | bytes 2359328 | tf_op jit(solution)/shard_map/ppermute | solution.py:14
  232.2 4.4 %select_convert_fusion.1 = bf16[768,768]{0,1:T(8,128)(2,1)S(1)} fusion(bf16[1536,768]{1,0:T(8,128)(2,1)} %fusion.3, bf16[1536,768]{1,0:T(8,128)(2,1)} %collective-permute-done.2, pred[]{:T(512)S(6)} %and.26), kind=kOutput, calls=%fused_computation.7 | convolution fusion | flops 1813708800 | bytes 5898241 | tf_op jit(solution)/shard_map/dot_general | solution.py:49
  236.6 1.9 collective-permute-start.3
  238.5 45.7 %collective-permute-done = bf16[1536,768]{1,0:T(8,128)(2,1)} collective-permute-done((bf16[1536,768]{1,0:T(8,128)(2,1)}, bf16[1536,768]{1,0:T(8,128)(2,1)}, u32[]{:S(2)}, u32[]{:S(2)}) %collective-permute-start) | collective-permute-done | bytes 2359328 | tf_op jit(solution)/shard_map/ppermute | solution.py:14
  284.2 4.4 %select_convert_fusion.2 = bf16[768,768]{0,1:T(8,128)(2,1)S(1)} fusion(bf16[1536,768]{1,0:T(8,128)(2,1)} %fusion.3, bf16[1536,768]{1,0:T(8,128)(2,1)} %collective-permute-done, pred[]{:T(512)S(6)} %and.24), kind=kOutput, calls=%fused_computation.8 | convolution fusion | flops 1813708800 | bytes 5898241 | tf_op jit(solution)/shard_map/dot_general | solution.py:49
  290.1 1.9 collective-permute-start.1
  292.0 9.8 %collective-permute-start.6 = (bf16[768]{0:T(1024)(128)(2,1)S(1)}, bf16[768]{0:T(1024)(128)(2,1)S(1)}, u32[]{:S(2)}, u32[]{:S(2)}) collective-permute-start(bf16[768]{0:T(1024)(128)(2,1)S(1)} %copy-done.3), channel_id=1, source_target_pairs={{2,0},{3,1},{4,2},{5,3},{6,4},{7,5},{8,6},{9,7},{10,8},{11,9},{12,... | collective-permute-start | bytes 4616 | tf_op jit(solution)/shard_map/ppermute | solution.py:14
  301.9 1.9 collective-permute-start.5
  303.8 7.9 %collective-permute-start.4 = (bf16[768]{0:T(1024)(128)(2,1)S(1)}, bf16[768]{0:T(1024)(128)(2,1)}, u32[]{:S(2)}, u32[]{:S(2)}) collective-permute-start(bf16[768]{0:T(1024)(128)(2,1)S(1)} %copy-done.3), channel_id=1, source_target_pairs={{1,0},{2,1},{3,2},{4,3},{5,4},{6,5},{7,6},{8,7},{9,8},{10,9},{11,1... | collective-permute-start | bytes 4616 | tf_op jit(solution)/shard_map/ppermute | solution.py:14
  311.7 1.9 collective-permute-start.7
  319.5 3.2 collective-permute-done.7
  326.0 2.5 bitcast_dynamic-update-slice_fusion
  329.6 5.4 %constant_dynamic-update-slice_fusion.2 = (bf16[768,3840]{0,1:T(8,128)(2,1)}, bf16[768,768]{0,1:T(8,128)(2,1)S(1)}) fusion(bf16[768,3840]{0,1:T(8,128)(2,1)} %constant_dynamic-update-slice_fusion.3, bf16[1536,768]{1,0:T(8,128)(2,1)} %fusion.3, pred[]{:T(512)S(6)} %and.28), kind=kOutput, calls=%fused_computation.19 | convolution fusion | flops 1813708800 | bytes 7077889 | tf_op jit(solution)/shard_map/dot_general | solution.py:49
  335.8 1.6 fusion.6
  341.2 8.5 %all-reduce = f32[4]{0:T(128)S(1)} all-reduce(f32[4]{0:T(128)S(1)} %dynamic-update-slice), channel_id=1, replica_groups=mesh['row_0'=4,'row_1'=2,'row_2'=2,'col_0'=4,'col_1'=4] {'row_0'}, use_global_device_ids=true, to_apply=%add | all-reduce | flops 4 | bytes 32
  353.0 4.9 %all-reduce.1 = f32[2]{0:T(128)S(1)} all-reduce(f32[2]{0:T(128)S(1)} %dynamic-update-slice.1), channel_id=1, replica_groups=mesh['row_0'=4,'row_1'=2,'row_2'=2,'col_0'=4,'col_1'=4] {'row_1'}, use_global_device_ids=true, to_apply=%add.1 | all-reduce | flops 2 | bytes 16
  361.0 2.4 all-reduce.2
  366.6 12.5 %all-reduce.3 = f32[4]{0:T(128)S(1)} all-reduce(f32[4]{0:T(128)S(1)} %dynamic-update-slice.3), channel_id=1, replica_groups=mesh['row_0'=4,'row_1'=2,'row_2'=2,'col_0'=4,'col_1'=4] {'col_0'}, use_global_device_ids=true, to_apply=%add.3 | all-reduce | flops 4 | bytes 32
  381.0 8.4 %copy.8 = bf16[768,3840]{1,0:T(8,128)(2,1)} copy(bf16[768,3840]{0,1:T(8,128)(2,1)} %constant_dynamic-update-slice_fusion) | data formatting | bytes 11796480
  389.4 12.5 %all-reduce.4 = f32[4]{0:T(128)S(1)} all-reduce(f32[4]{0:T(128)S(1)} %dynamic-update-slice.4), channel_id=1, replica_groups=mesh['row_0'=4,'row_1'=2,'row_2'=2,'col_0'=4,'col_1'=4] {'col_1'}, use_global_device_ids=true, to_apply=%add.4 | all-reduce | flops 4 | bytes 32
  (56 shorter events, 28.6 us)
Async XLA Ops:
  0.6 2.4 copy-start
  3.7 14.7 %copy-start.5 = (s32[256]{0:T(256)S(1)}, s32[256]{0:T(256)}, u32[]{:S(2)}) copy-start(s32[256]{0:T(256)} %param.5) | copy-start | bytes 3076
  5.7 226.5 %collective-permute-start.2 = (bf16[1536,768]{1,0:T(8,128)(2,1)}, bf16[1536,768]{1,0:T(8,128)(2,1)}, u32[]{:S(2)}, u32[]{:S(2)}) collective-permute-start(bf16[1536,768]{1,0:T(8,128)(2,1)} %fusion.3), channel_id=1, source_target_pairs={{1,0},{2,1},{3,2},{4,3},{5,4},{6,5},{7,6},{8,7},{9,8},{10,9},{11,1... | collective-permute-start | bytes 7077896 | tf_op jit(solution)/shard_map/ppermute | solution.py:14
  15.3 268.9 %collective-permute-start = (bf16[1536,768]{1,0:T(8,128)(2,1)}, bf16[1536,768]{1,0:T(8,128)(2,1)}, u32[]{:S(2)}, u32[]{:S(2)}) collective-permute-start(bf16[1536,768]{1,0:T(8,128)(2,1)} %fusion.3), channel_id=1, source_target_pairs={{2,0},{3,1},{4,2},{5,3},{6,4},{7,5},{8,6},{9,7},{10,8},{11,9},{12,... | collective-permute-start | bytes 7077896 | tf_op jit(solution)/shard_map/ppermute | solution.py:14
  236.6 87.9 %collective-permute-start.3 = (bf16[768,768]{0,1:T(8,128)(2,1)S(1)}, bf16[768,768]{0,1:T(8,128)(2,1)S(1)}, u32[]{:S(2)}, u32[]{:S(2)}) collective-permute-start(bf16[768,768]{0,1:T(8,128)(2,1)S(1)} %select_convert_fusion.1), channel_id=1, source_target_pairs={{0,1},{1,2},{2,3},{3,4},{4,5},{5,6},{6,7},{7,8},{8,9},{9,10},{10,1... | collective-permute-start | bytes 3538952 | tf_op jit(solution)/shard_map/ppermute | solution.py:14
  288.6 3.4 copy-start.3
  290.1 35.9 %collective-permute-start.1 = (bf16[768,768]{1,0:T(8,128)(2,1)}, bf16[768,768]{1,0:T(8,128)(2,1)}, u32[]{:S(2)}, u32[]{:S(2)}) collective-permute-start(bf16[768,768]{1,0:T(8,128)(2,1)} %copy.6), channel_id=1, source_target_pairs={{0,2},{1,3},{2,4},{3,5},{4,6},{5,7},{6,8},{7,9},{8,10},{9,11},{10,... | collective-permute-start | bytes 3538952 | tf_op jit(solution)/shard_map/ppermute | solution.py:14
  292.0 19.6 %collective-permute-start.6 = (bf16[768]{0:T(1024)(128)(2,1)S(1)}, bf16[768]{0:T(1024)(128)(2,1)S(1)}, u32[]{:S(2)}, u32[]{:S(2)}) collective-permute-start(bf16[768]{0:T(1024)(128)(2,1)S(1)} %copy-done.3), channel_id=1, source_target_pairs={{2,0},{3,1},{4,2},{5,3},{6,4},{7,5},{8,6},{9,7},{10,8},{11,9},{12,... | collective-permute-start | bytes 4616 | tf_op jit(solution)/shard_map/ppermute | solution.py:14
  301.9 16.9 %collective-permute-start.5 = (bf16[768]{0:T(1024)(128)(2,1)S(1)}, bf16[768]{0:T(1024)(128)(2,1)S(1)}, u32[]{:S(2)}, u32[]{:S(2)}) collective-permute-start(bf16[768]{0:T(1024)(128)(2,1)S(1)} %copy-done.3), channel_id=1, source_target_pairs={{0,1},{1,2},{2,3},{3,4},{4,5},{5,6},{6,7},{7,8},{8,9},{9,10},{10,1... | collective-permute-start | bytes 4616 | tf_op jit(solution)/shard_map/ppermute | solution.py:14
  303.8 15.0 %collective-permute-start.4 = (bf16[768]{0:T(1024)(128)(2,1)S(1)}, bf16[768]{0:T(1024)(128)(2,1)}, u32[]{:S(2)}, u32[]{:S(2)}) collective-permute-start(bf16[768]{0:T(1024)(128)(2,1)S(1)} %copy-done.3), channel_id=1, source_target_pairs={{1,0},{2,1},{3,2},{4,3},{5,4},{6,5},{7,6},{8,7},{9,8},{10,9},{11,1... | collective-permute-start | bytes 4616 | tf_op jit(solution)/shard_map/ppermute | solution.py:14
  311.7 11.0 %collective-permute-start.7 = (bf16[768]{0:T(1024)(128)(2,1)S(1)}, bf16[768]{0:T(1024)(128)(2,1)}, u32[]{:S(2)}, u32[]{:S(2)}) collective-permute-start(bf16[768]{0:T(1024)(128)(2,1)S(1)} %copy-done.3), channel_id=1, source_target_pairs={{0,2},{1,3},{2,4},{3,5},{4,6},{5,7},{6,8},{7,9},{8,10},{9,11},{10,... | collective-permute-start | bytes 4616 | tf_op jit(solution)/shard_map/ppermute | solution.py:14
  326.0 2.5 copy-start.1
  335.0 0.8 copy-start.2
  335.0 2.3 copy-start.4
